TPU v7x, 32 devices: a whole 2x2x4 slice. The times are simulated.
32 devices in a mesh: dp: 8 (over z, x), rep: 4 (over y, core).
Axes of the slice: x: 2, y: 2, z: 4, core: 2. Of those that a mesh axis runs over, the one named last changes fastest.
Arguments:
- tokens: bfloat16 [8192, 2048], P(('rep', 'dp')), parts along dimension 0, may hold values from -12 to 12
- router: bfloat16 [8192, 8], P('rep'), parts along dimension 0, may hold values from -12 to 12
- w_gate: bfloat16 [8, 2048, 768], P('dp'), may hold values from -0.125 to 0.125
- w_up: bfloat16 [8, 2048, 768], P('dp'), may hold values from -0.125 to 0.125
- w_down: bfloat16 [8, 768, 2048], P('dp'), may hold values from -0.21875 to 0.21875
- picks: int32 [32, 32], P(('rep', 'dp')), parts along dimension 0, may hold values from 0 to 2047, as said below
Outputs:
- combined: bfloat16 [8192, 2048], P(('rep', 'dp')), parts along dimension 0
There are 4 independent parts, one for each index of `rep`. A program takes and returns all parts, laid end to end along the dimension named above; an argument that names none is the same for every part. Nothing has to cross between parts.
Inputs may be any that keep to these rules, and one draw needn't show every extreme that they name: `picks`: row e holds 32 different tokens taken by expert e, sorted by the device that holds them (256 tokens each, in order); at most 6 of them lie among one device's tokens, and in every row exactly 6 lie among some device's tokens.
All inputs are finite; a program needn't handle non-finite values.
Results may differ from a plain program's by a relative error of at most 0.0062.
Values may be sent and summed in bfloat16 or wider, within the bound.
No kernel may reach another device: no remote copies, remote signals or barrier semaphores. Data moves between devices by JAX's collectives and lax.ppermute only.
A program may use at most 64 MiB of HBM per device.

v0:
```python
import jax
import jax.numpy as jnp
from jax import lax
from jax.sharding import PartitionSpec as P

MOST = 6


def feed_forward(buffer_rows, gate_values, gate_w, up_w, down_w):
    gate_act = jnp.dot(buffer_rows, gate_w, preferred_element_type=jnp.float32)
    up_act = jnp.dot(buffer_rows, up_w, preferred_element_type=jnp.float32)
    hidden = (gate_values.astype(jnp.float32)[:, None] * jax.nn.silu(gate_act) * up_act).astype(
        jnp.bfloat16
    )
    return jnp.dot(hidden, down_w, preferred_element_type=jnp.float32).astype(jnp.bfloat16)


def body(tokens, router, w_gate, w_up, w_down, picks):
    sources = lax.axis_size("dp")
    tok_dev = tokens.shape[0]
    width = tokens.shape[1]
    experts = router.shape[1]
    my_picks = picks[0]
    capacity = my_picks.shape[0]
    logits = jnp.dot(tokens, router, preferred_element_type=jnp.float32)
    shares = jax.nn.softmax(logits, axis=1)
    source_of = my_picks // tok_dev
    block_ids = jnp.arange(sources, dtype=jnp.int32)
    counts = jnp.sum((source_of[None, :] == block_ids[:, None]).astype(jnp.int32), axis=1)
    starts = jnp.cumsum(counts) - counts
    slot_pos = jnp.arange(MOST, dtype=jnp.int32)
    within = jnp.arange(capacity, dtype=jnp.int32) - starts[source_of]
    flat_index = source_of * MOST + within
    position = jnp.clip(starts[:, None] + slot_pos[None, :], 0, capacity - 1)
    to_owner = jnp.where(
        slot_pos[None, :] < counts[:, None], my_picks[position] - block_ids[:, None] * tok_dev, -1
    )
    local_index = lax.all_to_all(to_owner, "dp", split_axis=0, concat_axis=0, tiled=True)
    live_slot = local_index >= 0
    safe_index = jnp.maximum(local_index, 0)
    send_rows = jnp.where(live_slot[:, :, None], tokens[safe_index], jnp.zeros((), tokens.dtype))
    columns = lax.all_to_all(
        shares.T.astype(jnp.bfloat16), "dp", split_axis=0, concat_axis=1, tiled=True
    ).astype(jnp.float32)
    gate_dense = (experts * columns[0][my_picks]).astype(jnp.bfloat16)
    received = lax.all_to_all(send_rows, "dp", split_axis=0, concat_axis=0, tiled=True)
    gate_flat = jnp.zeros((sources * MOST,), jnp.bfloat16).at[flat_index].set(gate_dense)
    buffer_rows = received.reshape(sources * MOST, width)
    expert_out = feed_forward(buffer_rows, gate_flat, w_gate[0], w_up[0], w_down[0])
    returned = lax.all_to_all(
        expert_out.reshape(sources, MOST, width), "dp", split_axis=0, concat_axis=0, tiled=True
    )
    onehot = (local_index.reshape(1, -1) == jnp.arange(tok_dev, dtype=jnp.int32)[:, None]).astype(
        jnp.bfloat16
    )
    combined = jnp.dot(
        onehot, returned.reshape(sources * MOST, width), preferred_element_type=jnp.float32
    )
    return combined.astype(jnp.bfloat16)


def solution(mesh):
    return jax.shard_map(
        body,
        mesh=mesh,
        in_specs=(
            P(("rep", "dp"), None),
            P("rep", None),
            P("dp", None, None),
            P("dp", None, None),
            P("dp", None, None),
            P(("rep", "dp"), None),
        ),
        out_specs=P(("rep", "dp"), None),
        check_vma=False,
    )
```

profile of v0, /device:TPU:0, one launch (start us, length us, event | category | flops | bytes accessed | tf_op | source)
XLA Modules:
  0.0 63.1 jit_solution(9098866142192156870)
XLA Ops:
  0.0 0.8 %fusion.32 = s32[32]{0:T(128)S(1)} fusion(s32[1,32]{1,0:T(1,128)} %param.11), kind=kLoop, calls=%fused_computation.61 | loop fusion | flops 480 | bytes 256 | tf_op jit(solution)/shard_map/eq | solution.py:29
  0.8 0.1 convert_reduce_fusion
  0.9 0.2 reduce-window.7
  1.2 0.1 reshape.319
  1.3 1.4 %gather_fusion = s32[48]{0:T(128)S(1)} fusion(s32[32]{0:T(128)} %bitcast.65, s32[1024]{0:T(1024)S(1)} %pad_clamp_fusion.3), kind=kCustom, calls=%fused_computation | custom fusion | bytes 576 | tf_op jit(solution)/shard_map/gather | solution.py:36
  2.8 0.7 %subtract_select_fusion = s32[8,1,6]{2,0,1:T(8,128)} fusion(s32[8,1,6]{2,0,1:T(8,128)S(1)} %gather.17, s32[8]{0:T(128)S(1)} %iota_multiply_fusion, s32[8]{0:T(128)S(1)} %convert_reduce_fusion), kind=kLoop, calls=%fused_computation.34 | loop fusion | flops 144 | bytes 448 | tf_op jit(solution)/shard_map/jit(_where)/select_n | solution.py:35
  3.5 7.3 %all-to-all-start = ((s32[8,1,6]{2,1,0:T(1,128)}), s32[8,1,6]{2,1,0:T(1,128)S(1)}, u32[]{:S(2)}, u32[]{:S(2)}) async-start(s32[8,1,6]{2,1,0:T(1,128)} %bitcast.4), calls=%async_computation | async-start | bytes 8192 | tf_op jit(solution)/shard_map/all_to_all | solution.py:38
  10.8 1.6 %fusion.36 = (f32[256]{0:T(256)S(1)}, f32[256,8]{0,1:T(8,128)S(1)}) fusion(bf16[256,2048]{1,0:T(8,128)(2,1)} %param.6, bf16[2048,8]{0,1:T(8,128)(2,1)S(1)} %copy-done.2), kind=kOutput, calls=%fused_computation.65 | convolution fusion | flops 8390400 | bytes 1090560 | tf_op jit(solution)/shard_map/dot_general | solution.py:25
  12.5 0.7 %gather_fusion.1 = s32[32]{0:T(128)S(1)} fusion(s32[8]{0:T(128)S(1)} %bitcast_subtract_fusion.1, s32[1024]{0:T(1024)S(1)} %get-tuple-element.11), kind=kCustom, calls=%fused_computation.1 | custom fusion | bytes 384 | tf_op jit(solution)/shard_map/gather | solution.py:32
  13.2 0.6 broadcast.287
  13.8 0.7 %reduce.4 = bf16[8,256]{1,0:T(8,128)(2,1)S(1)} reduce(bf16[8,1,256]{2,0,1:T(8,128)(2,1)S(1)} %fusion.27, bf16[]{:T(256)} %broadcast.287), dimensions={1}, to_apply=%copy.12.reduce_sub_computation | reduce | bytes 8194 | tf_op jit(solution)/shard_map/all_to_all | solution.py:42
  14.5 0.6 reshape.372
  15.1 2.1 %all-to-all-done = s32[8,1,6]{2,1,0:T(1,128)S(1)} async-done(((s32[8,1,6]{2,1,0:T(1,128)}), s32[8,1,6]{2,1,0:T(1,128)S(1)}, u32[]{:S(2)}, u32[]{:S(2)}) %all-to-all-start) | async-done | bytes 224 | tf_op jit(solution)/shard_map/all_to_all | solution.py:38
  17.2 3.9 %all-to-all-start.1 = ((bf16[8,2,128]{2,1,0:T(2,128)(2,1)}), bf16[8,2,128]{2,1,0:T(2,128)(2,1)S(1)}, u32[]{:S(2)}, u32[]{:S(2)}) async-start(bf16[8,2,128]{2,1,0:T(2,128)(2,1)} %reshape.372), calls=%async_computation.1 | async-start | bytes 8192 | tf_op jit(solution)/shard_map/all_to_all | solution.py:42
  21.2 2.2 %gather_fusion.3 = bf16[48,2048]{1,0:T(8,128)(2,1)S(1)} fusion(bf16[256,2048]{1,0:T(8,128)(2,1)} %param.6, s32[1024]{0:T(1024)S(1)} %pad_clamp_fusion), kind=kCustom, calls=%fused_computation.3 | custom fusion | bytes 393408 | tf_op jit(solution)/shard_map/gather | solution.py:41
  23.5 0.8 %reshape.342 = bf16[8,6,2048]{2,1,0:T(8,128)(2,1)} reshape(bf16[48,2048]{1,0:T(8,128)(2,1)S(1)} %gather_fusion.3) | data formatting | bytes 393216 | tf_op jit(solution)/shard_map/gather | solution.py:41
  24.2 1.7 %broadcast_select_fusion = bf16[8,6,2048]{2,1,0:T(8,128)(2,1)} fusion(bf16[8,6,2048]{2,1,0:T(8,128)(2,1)} %reshape.342, pred[8,6]{1,0:T(8,128)(4,1)S(1)} %compare_bitcast_fusion), kind=kLoop, calls=%fused_computation.15 | loop fusion | flops 98304 | bytes 393264 | tf_op jit(solution)/shard_map/jit(_where)/select_n | solution.py:41
  26.0 1.6 %all-to-all-done.1 = bf16[8,2,128]{2,1,0:T(2,128)(2,1)S(1)} async-done(((bf16[8,2,128]{2,1,0:T(2,128)(2,1)}), bf16[8,2,128]{2,1,0:T(2,128)(2,1)S(1)}, u32[]{:S(2)}, u32[]{:S(2)}) %all-to-all-start.1) | async-done | bytes 4128 | tf_op jit(solution)/shard_map/all_to_all | solution.py:42
  27.6 4.4 %all-to-all-start.2 = ((bf16[8,6,2048]{2,1,0:T(8,128)(2,1)}), bf16[8,6,2048]{2,1,0:T(8,128)(2,1)}, u32[]{:S(2)}, u32[]{:S(2)}) async-start(bf16[8,6,2048]{2,1,0:T(8,128)(2,1)} %broadcast_select_fusion), calls=%async_computation.2 | async-start | bytes 524288 | tf_op jit(solution)/shard_map/all_to_all | solution.py:46
  32.0 0.7 %gather_fusion.2 = f32[32]{0:T(128)S(1)} fusion(f32[2048]{0:T(1024)S(1)} %bitcast.66, s32[1024]{0:T(1024)S(1)} %get-tuple-element.10), kind=kCustom, calls=%fused_computation.2 | custom fusion | bytes 384 | tf_op jit(solution)/shard_map/gather | solution.py:45
  32.7 0.8 %scatter_custom_fusion = bf16[48]{0:T(256)(128)(2,1)S(1)} fusion(s32[32]{0:T(128)S(1)} %fusion.30, bf16[32]{0:T(256)(128)(2,1)S(1)} %multiply_convert_fusion, bf16[]{:T(256)} %constant.14.clone.1), kind=kCustom, calls=%fused_computation.62 | custom fusion | bytes 98 | tf_op jit(solution)/shard_map/scatter | solution.py:47
  33.5 6.8 %all-to-all-done.2 = bf16[8,6,2048]{2,1,0:T(8,128)(2,1)} async-done(((bf16[8,6,2048]{2,1,0:T(8,128)(2,1)}), bf16[8,6,2048]{2,1,0:T(8,128)(2,1)}, u32[]{:S(2)}, u32[]{:S(2)}) %all-to-all-start.2) | async-done | bytes 196640 | tf_op jit(solution)/shard_map/all_to_all | solution.py:46
  40.3 1.0 %reshape.313 = bf16[48,2048]{1,0:T(8,128)(2,1)S(1)} reshape(bf16[8,6,2048]{2,1,0:T(8,128)(2,1)} %all-to-all-done.2) | data formatting | bytes 393216 | tf_op jit(solution)/shard_map/reshape | solution.py:48
  41.3 3.2 %fusion.4 = f32[48,768]{1,0:T(8,128)} fusion(bf16[48,2048]{1,0:T(8,128)(2,1)S(1)} %reshape.313, bf16[1,2048,768]{2,1,0:T(8,128)(2,1)} %param.8), kind=kOutput, calls=%fused_computation.9 | convolution fusion | flops 150994944 | bytes 3489792 | tf_op jit(solution)/shard_map/dot_general | solution.py:10
  44.5 3.2 %fusion.6 = bf16[48,2048]{1,0:T(8,128)(2,1)S(1)} fusion(bf16[1,768,2048]{2,1,0:T(8,128)(2,1)S(1)} %copy-done, bf16[48,2048]{1,0:T(8,128)(2,1)S(1)} %reshape.313, bf16[1,2048,768]{2,1,0:T(8,128)(2,1)} %param.9, f32[48,768]{1,0:T(8,128)} %fusion.4, f32[48]{0:T(128)S(1)} %convert_element_type.40), kind=kOutput, calls=%fused_computation.12 | convolution fusion | flops 302346240 | bytes 6832320 | tf_op jit(solution)/shard_map/dot_general | solution.py:15
  47.7 0.8 %reshape.314 = bf16[8,6,2048]{2,1,0:T(8,128)(2,1)} reshape(bf16[48,2048]{1,0:T(8,128)(2,1)S(1)} %fusion.6) | data formatting | bytes 393216 | tf_op jit(solution)/shard_map/reshape | solution.py:51
  48.5 3.4 %all-to-all-start.3 = ((bf16[8,6,2048]{2,1,0:T(8,128)(2,1)}), bf16[8,6,2048]{2,1,0:T(8,128)(2,1)S(1)}, u32[]{:S(2)}, u32[]{:S(2)}) async-start(bf16[8,6,2048]{2,1,0:T(8,128)(2,1)} %reshape.314), calls=%async_computation.3 | async-start | bytes 524288 | tf_op jit(solution)/shard_map/all_to_all | solution.py:50
  51.9 0.6 broadcast.285
  52.5 0.7 %reduce.3 = s32[8,6]{1,0:T(8,128)S(1)} reduce(s32[8,1,6]{2,1,0:T(1,128)S(1)} %all-to-all-done, s32[]{:T(128)} %broadcast.285), dimensions={1}, to_apply=%all_to_all.20.reduce_sub_computation.3 | reduce | bytes 388 | tf_op jit(solution)/shard_map/all_to_all | solution.py:38
  53.3 6.8 %all-to-all-done.3 = bf16[8,6,2048]{2,1,0:T(8,128)(2,1)S(1)} async-done(((bf16[8,6,2048]{2,1,0:T(8,128)(2,1)}), bf16[8,6,2048]{2,1,0:T(8,128)(2,1)S(1)}, u32[]{:S(2)}, u32[]{:S(2)}) %all-to-all-start.3) | async-done | bytes 196640 | tf_op jit(solution)/shard_map/all_to_all | solution.py:50
  60.1 0.7 %reshape.315 = bf16[48,2048]{1,0:T(8,128)(2,1)} reshape(bf16[8,6,2048]{2,1,0:T(8,128)(2,1)S(1)} %all-to-all-done.3) | data formatting | bytes 393216 | tf_op jit(solution)/shard_map/reshape | solution.py:57
  60.8 2.3 %convolution_convert_fusion = bf16[256,2048]{1,0:T(8,128)(2,1)} fusion(bf16[48,2048]{1,0:T(8,128)(2,1)} %reshape.315, s32[48]{0:T(128)S(1)} %eq.34), kind=kOutput, calls=%fused_computation.11 | convolution fusion | flops 50868224 | bytes 1245376 | tf_op jit(solution)/shard_map/dot_general | solution.py:56
  (25 shorter events, 0.5 us)
Async XLA Ops:
  0.0 44.5 %copy-start = (bf16[1,768,2048]{2,1,0:T(8,128)(2,1)S(1)}, bf16[1,768,2048]{2,1,0:T(8,128)(2,1)}, u32[]{:S(2)}) copy-start(bf16[1,768,2048]{2,1,0:T(8,128)(2,1)} %param.10) | copy-start | bytes 9437188
  0.0 10.8 %copy-start.1 = (s32[1,32]{1,0:T(1,128)S(1)}, s32[1,32]{1,0:T(1,128)}, u32[]{:S(2)}) copy-start(s32[1,32]{1,0:T(1,128)} %param.11) | copy-start | bytes 388
  0.0 10.8 %copy-start.2 = (bf16[2048,8]{0,1:T(8,128)(2,1)S(1)}, bf16[2048,8]{0,1:T(8,128)(2,1)}, u32[]{:S(2)}) copy-start(bf16[2048,8]{0,1:T(8,128)(2,1)} %param.7) | copy-start | bytes 98308
  3.5 13.7 %all-to-all-start = ((s32[8,1,6]{2,1,0:T(1,128)}), s32[8,1,6]{2,1,0:T(1,128)S(1)}, u32[]{:S(2)}, u32[]{:S(2)}) async-start(s32[8,1,6]{2,1,0:T(1,128)} %bitcast.4), calls=%async_computation | async-start | bytes 8192 | tf_op jit(solution)/shard_map/all_to_all | solution.py:38
  17.2 10.4 %all-to-all-start.1 = ((bf16[8,2,128]{2,1,0:T(2,128)(2,1)}), bf16[8,2,128]{2,1,0:T(2,128)(2,1)S(1)}, u32[]{:S(2)}, u32[]{:S(2)}) async-start(bf16[8,2,128]{2,1,0:T(2,128)(2,1)} %reshape.372), calls=%async_computation.1 | async-start | bytes 8192 | tf_op jit(solution)/shard_map/all_to_all | solution.py:42
  27.6 12.7 %all-to-all-start.2 = ((bf16[8,6,2048]{2,1,0:T(8,128)(2,1)}), bf16[8,6,2048]{2,1,0:T(8,128)(2,1)}, u32[]{:S(2)}, u32[]{:S(2)}) async-start(bf16[8,6,2048]{2,1,0:T(8,128)(2,1)} %broadcast_select_fusion), calls=%async_computation.2 | async-start | bytes 524288 | tf_op jit(solution)/shard_map/all_to_all | solution.py:46
  48.5 11.6 %all-to-all-start.3 = ((bf16[8,6,2048]{2,1,0:T(8,128)(2,1)}), bf16[8,6,2048]{2,1,0:T(8,128)(2,1)S(1)}, u32[]{:S(2)}, u32[]{:S(2)}) async-start(bf16[8,6,2048]{2,1,0:T(8,128)(2,1)} %reshape.314), calls=%async_computation.3 | async-start | bytes 524288 | tf_op jit(solution)/shard_map/all_to_all | solution.py:50
where the time goes:
time: 63.7 us; the launch traced here: 63.1 us
  starting transfers between devices  19 us (30%)
  waiting for transfers between devices  17.3 us (27%)
  local copies, waits for them, and re-layouts  11.3 us (18%)
  matrix products  10.3 us (16%)
  other arithmetic  5.13 us (8%)
    all_to_all x1, starting transfers between devices, body(): lax.all_to_all(to_owner, 'dp', split_axis=0, concat_axis=0, tiled=True)  7.29 us
    all_to_all x1, waiting for transfers between devices, body(): lax.all_to_all(send_rows, 'dp', split_axis=0, concat_axis=0, tiled=True)  6.8 us
    all_to_all x1, waiting for transfers between devices, body(): lax.all_to_all(expert_out.reshape(sources, MOST, width), 'dp', split_axis...  6.78 us
    all_to_all x1, starting transfers between devices, body(): lax.all_to_all(send_rows, 'dp', split_axis=0, concat_axis=0, tiled=True)  4.37 us
    all_to_all x1, starting transfers between devices, body(): lax.all_to_all(shares.T.astype(jnp.bfloat16), 'dp', split_axis=0, concat_...  3.9 us
    all_to_all x1, starting transfers between devices, body(): lax.all_to_all(expert_out.reshape(sources, MOST, width), 'dp', split_axis...  3.41 us
    dot_general x1, matrix products, feed_forward(): jnp.dot(hidden, down_w, preferred_element_type=jnp.float32)  3.19 us
    dot_general x1, matrix products, feed_forward(): gate_act = jnp.dot(buffer_rows, gate_w, preferred_element_type=jnp.float32)  3.18 us
  transfers between devices with their start and end apart: 4, of which 4 were waited for; matrix products, arithmetic and copies ran while one was open for 19% of the time, Pallas kernels for 0%

commit v1 on v0

--- a/solution.py
+++ b/solution.py
@@ -1,9 +1,26 @@
+import functools
 import jax
 import jax.numpy as jnp
 from jax import lax
 from jax.sharding import PartitionSpec as P
+from jax.lax import axis_index, axis_size, ppermute
 
 MOST = 6
+
+
+def patch_update(unit, group_axis):
+    work_now, fresh = (axis_size(group_axis), axis_index(group_axis))
+    state_now = unit.shape[0] // work_now
+    mixed_arr = jnp.roll(unit, shift=-fresh * state_now, axis=0)
+    pages = [lax.slice_in_dim(mixed_arr, 0, state_now, axis=0)]
+    for kk in [*range(1, work_now)]:
+        top = lax.slice_in_dim(mixed_arr, kk * state_now, (kk + 1) * state_now, axis=0)
+        pages.append(ppermute(top, group_axis, [(j, (j + kk) % work_now) for j in range(work_now)]))
+    earlier = jnp.concatenate(pages[::-1], axis=0)
+    return jnp.roll(earlier, (fresh + 1) * pages[0].shape[0], axis=0)
+
+
+_track_chunk = functools.partial(patch_update, group_axis="dp")
 
 
 def feed_forward(buffer_rows, gate_values, gate_w, up_w, down_w):
@@ -35,7 +52,7 @@
     to_owner = jnp.where(
         slot_pos[None, :] < counts[:, None], my_picks[position] - block_ids[:, None] * tok_dev, -1
     )
-    local_index = lax.all_to_all(to_owner, "dp", split_axis=0, concat_axis=0, tiled=True)
+    local_index = _track_chunk(to_owner)
     live_slot = local_index >= 0
     safe_index = jnp.maximum(local_index, 0)
     send_rows = jnp.where(live_slot[:, :, None], tokens[safe_index], jnp.zeros((), tokens.dtype))

time: 63.7 us -> 70.9 us (1.11)
  starting transfers between devices: 19 us -> 28.4 us
  other arithmetic: 5.13 us -> 3.81 us
    ppermute x0 -> x7, starting transfers between devices: none -> 16.3 us  [patch_update(): ppermute(top, group_axis, [(j, (j + kk) % work_now) for j in range(work_n...]
    all_to_all x1 -> x0, starting transfers between devices: 7.29 us -> none  [body(): lax.all_to_all(to_owner, 'dp', split_axis=0, concat_axis=0, tiled=True)]
    ppermute x0 -> x7, waiting for transfers between devices: none -> 2.11 us  [patch_update(): ppermute(top, group_axis, [(j, (j + kk) % work_now) for j in range(work_n...]
    all_to_all x1 -> x0, waiting for transfers between devices: 2.1 us -> none  [body(): lax.all_to_all(to_owner, 'dp', split_axis=0, concat_axis=0, tiled=True)]
    all_to_all x1, waiting for transfers between devices: 1.63 us -> 0.01 us  [body(): lax.all_to_all(shares.T.astype(jnp.bfloat16), 'dp', split_axis=0, concat_...]
    all_to_all x1, waiting for transfers between devices: 6.78 us -> 8.08 us  [body(): lax.all_to_all(expert_out.reshape(sources, MOST, width), 'dp', split_axis...]
    all_to_all x1, starting transfers between devices: 4.37 us -> 5.43 us  [body(): lax.all_to_all(send_rows, 'dp', split_axis=0, concat_axis=0, tiled=True)]
  transfers between devices with their start and end apart: 4 -> 10, of which waited for: 4 -> 3; matrix products, arithmetic and copies ran while one was open for 19% -> 15% of each run, Pallas kernels for 0% -> 0%
where the time goes in v1:
time: 70.9 us; the launch traced here: 70.3 us
  starting transfers between devices  28.4 us (40%)
  waiting for transfers between devices  17 us (24%)
  local copies, waits for them, and re-layouts  10.6 us (15%)
  matrix products  10.3 us (15%)
  other arithmetic  3.81 us (5%)
    ppermute x7, starting transfers between devices, patch_update(): ppermute(top, group_axis, [(j, (j + kk) % work_now) for j in range(work_n...  16.3 us
    all_to_all x1, waiting for transfers between devices, body(): lax.all_to_all(expert_out.reshape(sources, MOST, width), 'dp', split_axis...  8.08 us
    all_to_all x1, waiting for transfers between devices, body(): lax.all_to_all(send_rows, 'dp', split_axis=0, concat_axis=0, tiled=True)  6.8 us
    all_to_all x1, starting transfers between devices, body(): lax.all_to_all(send_rows, 'dp', split_axis=0, concat_axis=0, tiled=True)  5.43 us
    all_to_all x1, starting transfers between devices, body(): lax.all_to_all(expert_out.reshape(sources, MOST, width), 'dp', split_axis...  3.41 us
    all_to_all x1, starting transfers between devices, body(): lax.all_to_all(shares.T.astype(jnp.bfloat16), 'dp', split_axis=0, concat_...  3.26 us
    dot_general x1, matrix products, feed_forward(): jnp.dot(hidden, down_w, preferred_element_type=jnp.float32)  3.2 us
    dot_general x1, matrix products, feed_forward(): gate_act = jnp.dot(buffer_rows, gate_w, preferred_element_type=jnp.float32)  3.18 us
  transfers between devices with their start and end apart: 10, of which 3 were waited for; matrix products, arithmetic and copies ran while one was open for 15% of the time, Pallas kernels for 0%

profile of v1, /device:TPU:0, one launch (start us, length us, event | category | flops | bytes accessed | tf_op | source)
XLA Modules:
  0.0 70.3 jit_solution(13822636822109079678)
XLA Ops:
  0.0 0.8 %fusion.34 = s32[32]{0:T(128)S(1)} fusion(s32[1,32]{1,0:T(1,128)} %param.13), kind=kLoop, calls=%fused_computation.67 | loop fusion | flops 480 | bytes 256 | tf_op jit(solution)/shard_map/eq | solution.py:46
  1.0 0.2 reduce-window.7
  1.3 1.4 %gather_fusion = s32[48]{0:T(128)S(1)} fusion(s32[32]{0:T(128)} %bitcast.58, s32[1024]{0:T(1024)S(1)} %pad_clamp_fusion.3), kind=kCustom, calls=%fused_computation | custom fusion | bytes 576 | tf_op jit(solution)/shard_map/gather | solution.py:53
  3.0 3.0 %collective-permute-start.6 = (s32[1,6]{1,0:T(1,128)S(1)}, s32[1,6]{1,0:T(1,128)S(1)}, u32[]{:S(2)}, u32[]{:S(2)}) collective-permute-start(s32[1,6]{1,0:T(1,128)S(1)} %get-tuple-element.11), channel_id=1, source_target_pairs={{0,4},{4,8},{8,12},{12,16},{16,20},{20,24},{24,28},{28,0},{1,5},{5... | collective-permute-start | bytes 80 | tf_op jit(solution)/shard_map/ppermute | solution.py:18
  6.0 1.6 %collective-permute-start.5 = (s32[1,6]{1,0:T(1,128)S(1)}, s32[1,6]{1,0:T(1,128)S(1)}, u32[]{:S(2)}, u32[]{:S(2)}) collective-permute-start(s32[1,6]{1,0:T(1,128)S(1)} %get-tuple-element.12), channel_id=1, source_target_pairs={{0,8},{4,12},{8,16},{12,20},{16,24},{20,28},{24,0},{28,4},{1,9},{5... | collective-permute-start | bytes 80 | tf_op jit(solution)/shard_map/ppermute | solution.py:18
  7.6 2.6 %collective-permute-start.4 = (s32[1,6]{1,0:T(1,128)S(1)}, s32[1,6]{1,0:T(1,128)S(1)}, u32[]{:S(2)}, u32[]{:S(2)}) collective-permute-start(s32[1,6]{1,0:T(1,128)S(1)} %get-tuple-element.13), channel_id=1, source_target_pairs={{0,12},{4,16},{8,20},{12,24},{16,28},{20,0},{24,4},{28,8},{1,13},{... | collective-permute-start | bytes 80 | tf_op jit(solution)/shard_map/ppermute | solution.py:18
  10.1 1.2 %collective-permute-start.3 = (s32[1,6]{1,0:T(1,128)S(1)}, s32[1,6]{1,0:T(1,128)S(1)}, u32[]{:S(2)}, u32[]{:S(2)}) collective-permute-start(s32[1,6]{1,0:T(1,128)S(1)} %get-tuple-element.14), channel_id=1, source_target_pairs={{0,16},{4,20},{8,24},{12,28},{16,0},{20,4},{24,8},{28,12},{1,17},{... | collective-permute-start | bytes 80 | tf_op jit(solution)/shard_map/ppermute | solution.py:18
  11.4 2.6 %collective-permute-start.2 = (s32[1,6]{1,0:T(1,128)S(1)}, s32[1,6]{1,0:T(1,128)S(1)}, u32[]{:S(2)}, u32[]{:S(2)}) collective-permute-start(s32[1,6]{1,0:T(1,128)S(1)} %get-tuple-element.15), channel_id=1, source_target_pairs={{0,20},{4,24},{8,28},{12,0},{16,4},{20,8},{24,12},{28,16},{1,21},{... | collective-permute-start | bytes 80 | tf_op jit(solution)/shard_map/ppermute | solution.py:18
  14.0 1.6 %fusion.40 = (f32[256]{0:T(256)S(1)}, f32[256,8]{0,1:T(8,128)S(1)}) fusion(bf16[256,2048]{1,0:T(8,128)(2,1)} %param.8, bf16[2048,8]{0,1:T(8,128)(2,1)S(1)} %copy-done.2), kind=kOutput, calls=%fused_computation.72 | convolution fusion | flops 8390400 | bytes 1090560 | tf_op jit(solution)/shard_map/dot_general | solution.py:42
  15.7 0.5 broadcast.240
  16.2 0.6 reduce
  16.8 0.6 reshape.287
  17.4 3.3 %all-to-all-start = ((bf16[8,2,128]{2,1,0:T(2,128)(2,1)}), bf16[8,2,128]{2,1,0:T(2,128)(2,1)S(1)}, u32[]{:S(2)}, u32[]{:S(2)}) async-start(bf16[8,2,128]{2,1,0:T(2,128)(2,1)} %reshape.287), calls=%async_computation | async-start | bytes 8192 | tf_op jit(solution)/shard_map/all_to_all | solution.py:59
  20.8 0.7 gather_fusion.1
  21.5 3.8 %collective-permute-start.1 = (s32[1,6]{1,0:T(1,128)S(1)}, s32[1,6]{1,0:T(1,128)S(1)}, u32[]{:S(2)}, u32[]{:S(2)}) collective-permute-start(s32[1,6]{1,0:T(1,128)S(1)} %get-tuple-element.16), channel_id=1, source_target_pairs={{0,24},{4,28},{8,0},{12,4},{16,8},{20,12},{24,16},{28,20},{1,25},{... | collective-permute-start | bytes 80 | tf_op jit(solution)/shard_map/ppermute | solution.py:18
  25.2 1.5 %collective-permute-start = (s32[1,6]{1,0:T(1,128)S(1)}, s32[1,6]{1,0:T(1,128)S(1)}, u32[]{:S(2)}, u32[]{:S(2)}) collective-permute-start(s32[1,6]{1,0:T(1,128)S(1)} %get-tuple-element.17), channel_id=1, source_target_pairs={{0,28},{4,0},{8,4},{12,8},{16,12},{20,16},{24,20},{28,24},{1,29},{... | collective-permute-start | bytes 80 | tf_op jit(solution)/shard_map/ppermute | solution.py:18
  26.7 2.1 %collective-permute-done = s32[1,6]{1,0:T(1,128)S(1)} collective-permute-done((s32[1,6]{1,0:T(1,128)S(1)}, s32[1,6]{1,0:T(1,128)S(1)}, u32[]{:S(2)}, u32[]{:S(2)}) %collective-permute-start) | collective-permute-done | bytes 56 | tf_op jit(solution)/shard_map/ppermute | solution.py:18
  29.0 2.2 %gather_fusion.3 = bf16[48,2048]{1,0:T(8,128)(2,1)S(1)} fusion(bf16[256,2048]{1,0:T(8,128)(2,1)} %param.8, s32[1024]{0:T(1024)S(1)} %pad_clamp_fusion), kind=kCustom, calls=%fused_computation.3 | custom fusion | bytes 393408 | tf_op jit(solution)/shard_map/gather | solution.py:58
  31.2 0.8 %reshape.267 = bf16[8,6,2048]{2,1,0:T(8,128)(2,1)} reshape(bf16[48,2048]{1,0:T(8,128)(2,1)S(1)} %gather_fusion.3) | data formatting | bytes 393216 | tf_op jit(solution)/shard_map/gather | solution.py:58
  32.0 1.7 %broadcast_select_fusion = bf16[8,6,2048]{2,1,0:T(8,128)(2,1)} fusion(bf16[8,6,2048]{2,1,0:T(8,128)(2,1)} %reshape.267, pred[8,6]{1,0:T(8,128)(4,1)S(1)} %get-tuple-element.8), kind=kLoop, calls=%fused_computation.15 | loop fusion | flops 98304 | bytes 393264 | tf_op jit(solution)/shard_map/jit(_where)/select_n | solution.py:58
  33.7 5.4 %all-to-all-start.1 = ((bf16[8,6,2048]{2,1,0:T(8,128)(2,1)}), bf16[8,6,2048]{2,1,0:T(8,128)(2,1)}, u32[]{:S(2)}, u32[]{:S(2)}) async-start(bf16[8,6,2048]{2,1,0:T(8,128)(2,1)} %broadcast_select_fusion), calls=%async_computation.1 | async-start | bytes 524288 | tf_op jit(solution)/shard_map/all_to_all | solution.py:63
  39.2 0.7 gather_fusion.2
  39.9 0.8 %scatter_custom_fusion = bf16[48]{0:T(256)(128)(2,1)S(1)} fusion(s32[32]{0:T(128)S(1)} %fusion.32, bf16[32]{0:T(256)(128)(2,1)S(1)} %multiply_convert_fusion, bf16[]{:T(256)} %constant.67.clone.1), kind=kCustom, calls=%fused_computation.68 | custom fusion | bytes 98 | tf_op jit(solution)/shard_map/scatter | solution.py:64
  40.7 6.8 %all-to-all-done.1 = bf16[8,6,2048]{2,1,0:T(8,128)(2,1)} async-done(((bf16[8,6,2048]{2,1,0:T(8,128)(2,1)}), bf16[8,6,2048]{2,1,0:T(8,128)(2,1)}, u32[]{:S(2)}, u32[]{:S(2)}) %all-to-all-start.1) | async-done | bytes 196640 | tf_op jit(solution)/shard_map/all_to_all | solution.py:63
  47.5 1.0 %reshape.238 = bf16[48,2048]{1,0:T(8,128)(2,1)S(1)} reshape(bf16[8,6,2048]{2,1,0:T(8,128)(2,1)} %all-to-all-done.1) | data formatting | bytes 393216 | tf_op jit(solution)/shard_map/reshape | solution.py:65
  48.5 3.2 %fusion.4 = f32[48,768]{1,0:T(8,128)} fusion(bf16[48,2048]{1,0:T(8,128)(2,1)S(1)} %reshape.238, bf16[1,2048,768]{2,1,0:T(8,128)(2,1)} %param.10), kind=kOutput, calls=%fused_computation.9 | convolution fusion | flops 150994944 | bytes 3489792 | tf_op jit(solution)/shard_map/dot_general | solution.py:27
  51.7 3.2 %fusion.6 = bf16[48,2048]{1,0:T(8,128)(2,1)S(1)} fusion(bf16[1,768,2048]{2,1,0:T(8,128)(2,1)S(1)} %copy-done, bf16[48,2048]{1,0:T(8,128)(2,1)S(1)} %reshape.238, bf16[1,2048,768]{2,1,0:T(8,128)(2,1)} %param.11, f32[48,768]{1,0:T(8,128)} %fusion.4, f32[48]{0:T(128)S(1)} %convert_element_type.40), kind=kOutput, calls=%fused_computation.12 | convolution fusion | flops 302346240 | bytes 6832320 | tf_op jit(solution)/shard_map/dot_general | solution.py:32
  54.9 0.8 %reshape.239 = bf16[8,6,2048]{2,1,0:T(8,128)(2,1)} reshape(bf16[48,2048]{1,0:T(8,128)(2,1)S(1)} %fusion.6) | data formatting | bytes 393216 | tf_op jit(solution)/shard_map/reshape | solution.py:68
  55.7 3.4 %all-to-all-start.2 = ((bf16[8,6,2048]{2,1,0:T(8,128)(2,1)}), bf16[8,6,2048]{2,1,0:T(8,128)(2,1)S(1)}, u32[]{:S(2)}, u32[]{:S(2)}) async-start(bf16[8,6,2048]{2,1,0:T(8,128)(2,1)} %reshape.239), calls=%async_computation.2 | async-start | bytes 524288 | tf_op jit(solution)/shard_map/all_to_all | solution.py:67
  59.2 8.1 %all-to-all-done.2 = bf16[8,6,2048]{2,1,0:T(8,128)(2,1)S(1)} async-done(((bf16[8,6,2048]{2,1,0:T(8,128)(2,1)}), bf16[8,6,2048]{2,1,0:T(8,128)(2,1)S(1)}, u32[]{:S(2)}, u32[]{:S(2)}) %all-to-all-start.2) | async-done | bytes 196640 | tf_op jit(solution)/shard_map/all_to_all | solution.py:67
  67.3 0.7 %reshape.240 = bf16[48,2048]{1,0:T(8,128)(2,1)} reshape(bf16[8,6,2048]{2,1,0:T(8,128)(2,1)S(1)} %all-to-all-done.2) | data formatting | bytes 393216 | tf_op jit(solution)/shard_map/reshape | solution.py:74
  68.0 2.3 %convolution_convert_fusion = bf16[256,2048]{1,0:T(8,128)(2,1)} fusion(bf16[48,2048]{1,0:T(8,128)(2,1)} %reshape.240, s32[48]{0:T(128)S(1)} %eq.36), kind=kOutput, calls=%fused_computation.11 | convolution fusion | flops 50868224 | bytes 1245376 | tf_op jit(solution)/shard_map/dot_general | solution.py:73
  (38 shorter events, 0.8 us)
Async XLA Ops:
  0.0 51.7 %copy-start = (bf16[1,768,2048]{2,1,0:T(8,128)(2,1)S(1)}, bf16[1,768,2048]{2,1,0:T(8,128)(2,1)}, u32[]{:S(2)}) copy-start(bf16[1,768,2048]{2,1,0:T(8,128)(2,1)} %param.12) | copy-start | bytes 9437188
  0.0 20.7 %copy-start.1 = (s32[1,32]{1,0:T(1,128)S(1)}, s32[1,32]{1,0:T(1,128)}, u32[]{:S(2)}) copy-start(s32[1,32]{1,0:T(1,128)} %param.13) | copy-start | bytes 388
  0.0 14.0 %copy-start.2 = (bf16[2048,8]{0,1:T(8,128)(2,1)S(1)}, bf16[2048,8]{0,1:T(8,128)(2,1)}, u32[]{:S(2)}) copy-start(bf16[2048,8]{0,1:T(8,128)(2,1)} %param.9) | copy-start | bytes 98308
  3.0 18.5 %collective-permute-start.6 = (s32[1,6]{1,0:T(1,128)S(1)}, s32[1,6]{1,0:T(1,128)S(1)}, u32[]{:S(2)}, u32[]{:S(2)}) collective-permute-start(s32[1,6]{1,0:T(1,128)S(1)} %get-tuple-element.11), channel_id=1, source_target_pairs={{0,4},{4,8},{8,12},{12,16},{16,20},{20,24},{24,28},{28,0},{1,5},{5... | collective-permute-start | bytes 80 | tf_op jit(solution)/shard_map/ppermute | solution.py:18
  6.0 19.3 %collective-permute-start.5 = (s32[1,6]{1,0:T(1,128)S(1)}, s32[1,6]{1,0:T(1,128)S(1)}, u32[]{:S(2)}, u32[]{:S(2)}) collective-permute-start(s32[1,6]{1,0:T(1,128)S(1)} %get-tuple-element.12), channel_id=1, source_target_pairs={{0,8},{4,12},{8,16},{12,20},{16,24},{20,28},{24,0},{28,4},{1,9},{5... | collective-permute-start | bytes 80 | tf_op jit(solution)/shard_map/ppermute | solution.py:18
  7.6 19.1 %collective-permute-start.4 = (s32[1,6]{1,0:T(1,128)S(1)}, s32[1,6]{1,0:T(1,128)S(1)}, u32[]{:S(2)}, u32[]{:S(2)}) collective-permute-start(s32[1,6]{1,0:T(1,128)S(1)} %get-tuple-element.13), channel_id=1, source_target_pairs={{0,12},{4,16},{8,20},{12,24},{16,28},{20,0},{24,4},{28,8},{1,13},{... | collective-permute-start | bytes 80 | tf_op jit(solution)/shard_map/ppermute | solution.py:18
  10.1 16.6 %collective-permute-start.3 = (s32[1,6]{1,0:T(1,128)S(1)}, s32[1,6]{1,0:T(1,128)S(1)}, u32[]{:S(2)}, u32[]{:S(2)}) collective-permute-start(s32[1,6]{1,0:T(1,128)S(1)} %get-tuple-element.14), channel_id=1, source_target_pairs={{0,16},{4,20},{8,24},{12,28},{16,0},{20,4},{24,8},{28,12},{1,17},{... | collective-permute-start | bytes 80 | tf_op jit(solution)/shard_map/ppermute | solution.py:18
  11.4 15.3 %collective-permute-start.2 = (s32[1,6]{1,0:T(1,128)S(1)}, s32[1,6]{1,0:T(1,128)S(1)}, u32[]{:S(2)}, u32[]{:S(2)}) collective-permute-start(s32[1,6]{1,0:T(1,128)S(1)} %get-tuple-element.15), channel_id=1, source_target_pairs={{0,20},{4,24},{8,28},{12,0},{16,4},{20,8},{24,12},{28,16},{1,21},{... | collective-permute-start | bytes 80 | tf_op jit(solution)/shard_map/ppermute | solution.py:18
  17.4 16.3 %all-to-all-start = ((bf16[8,2,128]{2,1,0:T(2,128)(2,1)}), bf16[8,2,128]{2,1,0:T(2,128)(2,1)S(1)}, u32[]{:S(2)}, u32[]{:S(2)}) async-start(bf16[8,2,128]{2,1,0:T(2,128)(2,1)} %reshape.287), calls=%async_computation | async-start | bytes 8192 | tf_op jit(solution)/shard_map/all_to_all | solution.py:59
  21.5 5.3 %collective-permute-start.1 = (s32[1,6]{1,0:T(1,128)S(1)}, s32[1,6]{1,0:T(1,128)S(1)}, u32[]{:S(2)}, u32[]{:S(2)}) collective-permute-start(s32[1,6]{1,0:T(1,128)S(1)} %get-tuple-element.16), channel_id=1, source_target_pairs={{0,24},{4,28},{8,0},{12,4},{16,8},{20,12},{24,16},{28,20},{1,25},{... | collective-permute-start | bytes 80 | tf_op jit(solution)/shard_map/ppermute | solution.py:18
  25.2 3.6 %collective-permute-start = (s32[1,6]{1,0:T(1,128)S(1)}, s32[1,6]{1,0:T(1,128)S(1)}, u32[]{:S(2)}, u32[]{:S(2)}) collective-permute-start(s32[1,6]{1,0:T(1,128)S(1)} %get-tuple-element.17), channel_id=1, source_target_pairs={{0,28},{4,0},{8,4},{12,8},{16,12},{20,16},{24,20},{28,24},{1,29},{... | collective-permute-start | bytes 80 | tf_op jit(solution)/shard_map/ppermute | solution.py:18
  33.7 13.8 %all-to-all-start.1 = ((bf16[8,6,2048]{2,1,0:T(8,128)(2,1)}), bf16[8,6,2048]{2,1,0:T(8,128)(2,1)}, u32[]{:S(2)}, u32[]{:S(2)}) async-start(bf16[8,6,2048]{2,1,0:T(8,128)(2,1)} %broadcast_select_fusion), calls=%async_computation.1 | async-start | bytes 524288 | tf_op jit(solution)/shard_map/all_to_all | solution.py:63
  55.7 11.6 %all-to-all-start.2 = ((bf16[8,6,2048]{2,1,0:T(8,128)(2,1)}), bf16[8,6,2048]{2,1,0:T(8,128)(2,1)S(1)}, u32[]{:S(2)}, u32[]{:S(2)}) async-start(bf16[8,6,2048]{2,1,0:T(8,128)(2,1)} %reshape.239), calls=%async_computation.2 | async-start | bytes 524288 | tf_op jit(solution)/shard_map/all_to_all | solution.py:67
